TPU v7x, 32 devices: a whole 2x2x4 slice. The times are simulated.
32 devices in a mesh: parts: 2 (over x), seq: 16 (over z, y, core).
Axes of the slice: x: 2, y: 2, z: 4, core: 2. Of those that a mesh axis runs over, the one named last changes fastest.
Arguments:
- token_ids: int32 [4, 4], P(None, 'parts'), parts along dimension 1, may hold values from 0 to 76031
- lengths: int32 [4], P('parts'), parts along dimension 0, may hold values from 24576 to 32768, as said below
- embed_table: bfloat16 [76032, 5120], P('seq'), may hold values from -6 to 6
- attn_gain: bfloat16 [5120], replicated, may hold values from 0.25 to 1.75
- w_qkv: bfloat16 [5120, 7168], P('seq'), may hold values from -0.125 to 0.125
- qkv_bias: float32 [7168], replicated, may hold values from -8 to 8
- cache_keys: bfloat16 [4, 32768, 1024], P('parts', 'seq'), parts along dimension 0, may hold values from -300 to 300
- cache_values: bfloat16 [4, 32768, 1024], P('parts', 'seq'), parts along dimension 0, may hold values from -6 to 6
- w_out: bfloat16 [5120, 5120], P(None, 'seq'), may hold values from -0.078125 to 0.078125
- mlp_gain: bfloat16 [5120], replicated, may hold values from 0.25 to 1.75
- w_gate: bfloat16 [5120, 16384], P(None, 'seq'), may hold values from -0.078125 to 0.078125
- w_up: bfloat16 [5120, 16384], P(None, 'seq'), may hold values from -0.078125 to 0.078125
- w_down: bfloat16 [16384, 5120], P('seq'), may hold values from -0.0625 to 0.0625
Outputs:
- attended: bfloat16 [4, 4, 5120], P(None, 'parts'), parts along dimension 1
- layer_out: bfloat16 [4, 4, 5120], P(None, 'parts', 'seq'), parts along dimension 1
There are 2 independent parts, one for each index of `parts`. A program takes and returns all parts, laid end to end along the dimension named above; an argument that names none is the same for every part. Nothing has to cross between parts.
Inputs may be any that keep to these rules, and one draw needn't show every extreme that they name: Cache positions lengths[b] and later are unused; the first prompt fills the whole cache of 32768 positions.
All inputs are finite; a program needn't handle non-finite values.
Results may differ from a plain program's by a relative error of at most 0.017.
The roundings to bfloat16 on the way count: a program that leaves them out, or rounds other values in their place, can miss the bound.
Values may be sent and summed in bfloat16 or wider, within the bound.
A program may use at most 192 MiB of HBM per device.

v0:
```python
import math
import jax
import jax.numpy as jnp
from jax import lax
from jax.sharding import PartitionSpec as P

HEADS = 40
KV_HEADS = 8
HEAD_DIM = 128
NORM_EPS = 1e-06
ROPE_BASE = 1000000.0
MASKED = -1e30


def joined_2(part, axis, combine):
    gathered = jax.tree.map(lambda a: lax.all_gather(a, axis), part)

    def take(source):
        return jax.tree.map(lambda a: lax.dynamic_index_in_dim(a, source, 0, False), gathered)

    return lax.fori_loop(
        1, lax.axis_size(axis), lambda source, state: combine(state, take(source)), take(0)
    )


def rms_normalize(rows, gain):
    mean_square = jnp.mean(rows * rows, axis=-1, keepdims=True)
    return (rows * lax.rsqrt(mean_square + NORM_EPS) * gain.astype(jnp.float32)).astype(
        jnp.bfloat16
    )


def rotate(vectors, positions):
    half_dim = vectors.shape[-1] // 2
    frequency = ROPE_BASE ** (-2.0 * jnp.arange(half_dim, dtype=jnp.float32) / vectors.shape[-1])
    angles = positions.astype(jnp.float32)[..., None, None] * frequency
    cosine = jnp.cos(angles)
    sine_part = jnp.sin(angles)
    widened = vectors.astype(jnp.float32)
    first_half = widened[..., :half_dim]
    second = widened[..., half_dim:]
    joined = jnp.concatenate(
        [first_half * cosine - second * sine_part, second * cosine + first_half * sine_part],
        axis=-1,
    )
    return joined.astype(jnp.bfloat16)


def combine_partials(earlier, latter):
    top_one, total_one, sum_one = earlier
    top_two, total_two, sum_two = latter
    joined_top = jnp.maximum(top_one, top_two)
    scale_one = jnp.exp(top_one - joined_top)
    scale_two = jnp.exp(top_two - joined_top)
    return (
        joined_top,
        total_one * scale_one + total_two * scale_two,
        sum_one * scale_one[..., None] + sum_two * scale_two[..., None],
    )


def body(
    token_ids,
    lengths,
    embed_table,
    attn_gain,
    w_qkv,
    qkv_bias,
    cache_keys,
    cache_values,
    w_out,
    mlp_gain,
    w_gate,
    w_up,
    w_down,
):
    rank = lax.axis_index("seq")
    step_count, batch_count = token_ids.shape
    model_width = embed_table.shape[1]
    vocab_rows = embed_table.shape[0]
    query_width = HEADS * HEAD_DIM
    key_width = KV_HEADS * HEAD_DIM
    group_size = HEADS // KV_HEADS
    local_ids = token_ids - rank * vocab_rows
    inside = (local_ids >= 0) & (local_ids < vocab_rows)
    picked = jnp.take(embed_table, jnp.clip(local_ids, 0, vocab_rows - 1), axis=0)
    partial_rows = jnp.where(inside[..., None], picked.astype(jnp.float32), 0.0)
    stream = lax.psum(partial_rows, "seq")
    normed = rms_normalize(stream, attn_gain).reshape(-1, model_width)
    feature_rows = w_qkv.shape[0]
    normed_local = lax.dynamic_slice_in_dim(normed, rank * feature_rows, feature_rows, 1)
    joint_partial = jnp.dot(normed_local, w_qkv, preferred_element_type=jnp.float32)
    joint_summed = lax.psum(joint_partial, "seq")
    joint = (joint_summed + qkv_bias).astype(jnp.bfloat16).reshape(step_count, batch_count, -1)
    query_part = joint[..., :query_width].reshape(step_count, batch_count, HEADS, HEAD_DIM)
    key_part = joint[..., query_width : query_width + key_width].reshape(
        step_count, batch_count, KV_HEADS, HEAD_DIM
    )
    value_part = joint[..., query_width + key_width :].reshape(
        step_count, batch_count, KV_HEADS, HEAD_DIM
    )
    positions = lengths[None, :] + jnp.arange(step_count, dtype=jnp.int32)[:, None]
    queries = rotate(query_part, positions)
    new_keys = rotate(key_part, positions)
    grouped = queries.reshape(step_count, batch_count, KV_HEADS, group_size, HEAD_DIM)
    score_scale = 1.0 / math.sqrt(HEAD_DIM)
    local_len = cache_keys.shape[1]
    key_blocks = cache_keys.reshape(batch_count, local_len, KV_HEADS, HEAD_DIM)
    value_blocks = cache_values.reshape(batch_count, local_len, KV_HEADS, HEAD_DIM)
    scores = (
        jnp.einsum("sbkgd,bpkd->bkgsp", grouped, key_blocks, preferred_element_type=jnp.float32)
        * score_scale
    )
    places = rank * local_len + jnp.arange(local_len, dtype=jnp.int32)
    valid = (places[None, :] < lengths[:, None])[:, None, None, None, :]
    masked = jnp.where(valid, scores, MASKED)
    local_top = jnp.max(masked, axis=-1)
    weights = jnp.where(valid, jnp.exp(masked - local_top[..., None]), 0.0)
    local_total = jnp.sum(weights, axis=-1)
    local_sum = jnp.einsum(
        "bkgsp,bpkd->bkgsd",
        weights.astype(jnp.bfloat16),
        value_blocks,
        preferred_element_type=jnp.float32,
    )
    merged_top, merged_total, merged_sum = joined_2(
        (local_top, local_total, local_sum), "seq", combine_partials
    )
    new_scores = (
        jnp.einsum("sbkgd,tbkd->bkgst", grouped, new_keys, preferred_element_type=jnp.float32)
        * score_scale
    )
    step_index = jnp.arange(step_count, dtype=jnp.int32)
    causal = step_index[:, None] >= step_index[None, :]
    new_masked = jnp.where(causal, new_scores, MASKED)
    final_top = jnp.maximum(merged_top, jnp.max(new_masked, axis=-1))
    rescale = jnp.exp(merged_top - final_top)
    new_weights = jnp.where(causal, jnp.exp(new_masked - final_top[..., None]), 0.0)
    final_total = merged_total * rescale + jnp.sum(new_weights, axis=-1)
    final_sum = merged_sum * rescale[..., None] + jnp.einsum(
        "bkgst,tbkd->bkgsd",
        new_weights.astype(jnp.bfloat16),
        value_part,
        preferred_element_type=jnp.float32,
    )
    attended = jnp.transpose(final_sum / final_total[..., None], (3, 0, 1, 2, 4))
    attended = attended.reshape(step_count, batch_count, query_width).astype(jnp.bfloat16)
    shard_cols = w_out.shape[1]
    projected = jnp.dot(
        attended.reshape(-1, query_width), w_out, preferred_element_type=jnp.float32
    )
    stream_shard = lax.dynamic_slice_in_dim(stream, rank * shard_cols, shard_cols, 2)
    mid_shard = stream_shard + projected.reshape(step_count, batch_count, shard_cols)
    squares = lax.psum(jnp.sum(mid_shard * mid_shard, axis=-1), "seq")
    row_scale = lax.rsqrt(squares / model_width + NORM_EPS)
    gain_shard = lax.dynamic_slice_in_dim(mlp_gain, rank * shard_cols, shard_cols, 0).astype(
        jnp.float32
    )
    normed_shard = (mid_shard * row_scale[..., None] * gain_shard).astype(jnp.bfloat16)
    normed_mid = lax.all_gather(normed_shard, "seq", axis=2, tiled=True)
    flat_rows = normed_mid.reshape(-1, model_width)
    gate = jnp.dot(flat_rows, w_gate, preferred_element_type=jnp.float32)
    upper = jnp.dot(flat_rows, w_up, preferred_element_type=jnp.float32)
    hidden = (jax.nn.silu(gate) * upper).astype(jnp.bfloat16)
    down_terms = jnp.dot(hidden, w_down, preferred_element_type=jnp.float32).reshape(
        step_count, batch_count, model_width
    )
    summed = lax.psum_scatter(down_terms, "seq", scatter_dimension=2, tiled=True)
    layer_out = (mid_shard + summed).astype(jnp.bfloat16)
    return (attended, layer_out)


def solution(mesh):
    return jax.shard_map(
        body,
        mesh=mesh,
        in_specs=(
            P(None, "parts"),
            P("parts"),
            P("seq", None),
            P(),
            P("seq", None),
            P(),
            P("parts", "seq", None),
            P("parts", "seq", None),
            P(None, "seq"),
            P(),
            P(None, "seq"),
            P(None, "seq"),
            P("seq", None),
        ),
        out_specs=(P(None, "parts", None), P(None, "parts", "seq")),
        check_vma=False,
    )
```

profile of v0, /device:TPU:0, one launch (start us, length us, event | category | flops | bytes accessed | tf_op | source)
XLA Modules:
  0.0 495.7 jit_solution(8823497209833906688)
XLA Ops:
  8.3 1.9 gather_fusion
  13.4 8.8 %copy.106 = bf16[512,8,8,128]{3,2,1,0:T(8,128)(2,1)} copy(bf16[512,8,8,128]{3,1,2,0:T(8,128)(2,1)} %bitcast.100) | data formatting | bytes 16777216
  22.2 7.1 %bitcast_bitcast_fusion.1 = bf16[2,2048,8,128,1]{3,2,1,0,4:T(8,128)(2,1)} fusion(bf16[2,2048,8,128]{3,2,1,0:T(8,128)(2,1)} %bitcast.97), kind=kLoop, calls=%fused_computation.12 | loop fusion | bytes 16777216 | tf_op jit(solution)/shard_map/reshape | solution.py:108
  29.3 8.8 %copy.107 = bf16[512,8,8,128]{3,2,1,0:T(8,128)(2,1)} copy(bf16[512,8,8,128]{3,1,2,0:T(8,128)(2,1)} %bitcast.101) | data formatting | bytes 16777216
  38.1 7.0 %bitcast_bitcast_fusion = bf16[2,2048,8,128,1]{3,2,1,0,4:T(8,128)(2,1)} fusion(bf16[2,2048,8,128]{3,2,1,0:T(8,128)(2,1)} %bitcast.98), kind=kLoop, calls=%fused_computation.11 | loop fusion | bytes 16777216 | tf_op jit(solution)/shard_map/reshape | solution.py:109
  45.2 57.9 %all-reduce.3.cloned.1.call-done = f32[4,2,5120]{2,1,0:T(2,128)} async-done(((f32[4,2,5120]{2,1,0:T(2,128)}), f32[4,2,5120]{2,1,0:T(2,128)}) %all-reduce.3.cloned.1.call-update) | async-done | bytes 163856 | tf_op jit(solution)/shard_map/psum | solution.py:88
  105.3 3.7 fusion.47
  109.4 90.0 %all-reduce.5.cloned.1.call-done = f32[8,7168]{1,0:T(8,128)} async-done(((f32[8,7168]{1,0:T(8,128)}), f32[8,7168]{1,0:T(8,128)}) %all-reduce.5.cloned.1.call-update) | async-done | bytes 229392 | tf_op jit(solution)/shard_map/psum | solution.py:93
  201.2 6.3 %bitcast_reduce_fusion = (f32[2,8,5,4]{2,3,1,0:T(4,128)S(1)}, f32[2,8,4,5,2048]{4,3,2,1,0:T(8,128)S(1)}) fusion(pred[2,2048]{1,0:T(4,128)(4,1)S(1)} %broadcast_compare_fusion, bf16[2,2048,8,128,1]{3,2,1,0,4:T(8,128)(2,1)} %bitcast_bitcast_fusion.1, bf16[4,2,8,5,64]{4,3,0,2,1:T(8,128)(2,1)S(1)} %copy.69, bf16[4,2,8,5,64]{4,3,0,2,1:T(8,128)(2,1)S(1)} %copy.68), kind=kOutput, calls=%fused_computation.18 | convolution fusion | flops 169901760 | bytes 11097344 | tf_op jit(solution)/shard_map/sbkgd,bpkd->bkgsp/dot_general | solution.py:111
  207.6 3.1 fusion.4
  212.5 3.6 fusion.13
  216.2 23.1 %all-gather.1 = f32[32,8,5,4]{1,3,2,0:T(4,128)S(1)} all-gather(f32[2,8,5,4]{1,3,2,0:T(4,128)S(1)} %copy.72), channel_id=3, replica_groups=mesh['parts'=2,'seq'=16] {'seq'}, dimensions={0}, use_global_device_ids=true | all-gather | bytes 21760 | tf_op jit(solution)/shard_map/all_gather | solution.py:16
  240.1 19.3 %all-gather = f32[32,8,5,4]{1,3,2,0:T(4,128)S(1)} all-gather(f32[2,8,5,4]{1,3,2,0:T(4,128)S(1)} %copy.71), channel_id=2, replica_groups=mesh['parts'=2,'seq'=16] {'seq'}, dimensions={0}, use_global_device_ids=true | all-gather | bytes 21760 | tf_op jit(solution)/shard_map/all_gather | solution.py:16
  261.1 2.3 fusion.60
  265.1 57.2 %while.19 = (s32[]{:T(128)}, f32[2,8,5,4]{1,3,2,0:T(4,128)S(1)}, f32[2,8,5,4]{1,3,2,0:T(4,128)S(1)}, f32[2,8,5,4,128]{4,3,2,1,0:T(4,128)}, f32[16,2,8,5,4]{2,4,3...) while((s32[]{:T(128)}, f32[2,8,5,4]{1,3,2,0:T(4,128)S(1)}, ...), condition=%wide.region_6.7_spmd, body=%wide.region_5.6_spmd.sunk | while | flops 124805 | bytes 837271 | solution.py:21
  267.0 1.8 fusion.72
  270.9 1.8 fusion.72
  274.7 1.8 fusion.72
  278.5 1.8 fusion.72
  286.1 1.8 fusion.72
  290.0 1.8 fusion.72
  293.8 1.8 fusion.72
  325.1 1.8 multiply_reduce_fusion.1
  327.0 30.7 %psum.23 = f32[4,2]{1,0:T(4,128)S(1)} all-reduce(f32[4,2]{1,0:T(4,128)S(1)} %get-tuple-element.245), channel_id=1, replica_groups=mesh['parts'=2,'seq'=16] {'seq'}, use_global_device_ids=true, to_apply=%region_10.11 | all-reduce | flops 8 | bytes 64 | tf_op jit(solution)/shard_map/psum | solution.py:154
  357.9 33.2 %all_gather.27 = bf16[4,2,5120]{0,1,2:T(2,128)(2,1)} all-gather(bf16[4,2,320]{0,1,2:T(2,128)(2,1)S(1)} %copy.85), channel_id=1, replica_groups=mesh['parts'=2,'seq'=16] {'seq'}, dimensions={2}, use_global_device_ids=true | all-gather | bytes 87040 | tf_op jit(solution)/shard_map/all_gather | solution.py:160
  391.2 5.2 %copy.86 = bf16[4,2,5120]{2,1,0:T(2,128)(2,1)S(1)} copy(bf16[4,2,5120]{0,1,2:T(2,128)(2,1)} %all_gather.27) | data formatting | bytes 163840 | tf_op jit(solution)/shard_map/all_gather | solution.py:160
  396.5 5.4 %fusion.61 = f32[8,1024]{1,0:T(8,128)S(1)} fusion(bf16[8,5120]{1,0:T(8,128)(2,1)S(1)} %reshape.133, bf16[5120,1024]{1,0:T(8,128)(2,1)} %param.25), kind=kOutput, calls=%fused_computation.105 | convolution fusion | flops 83886080 | bytes 10600448 | tf_op jit(solution)/shard_map/dot_general | solution.py:162
  401.9 9.8 %fusion.30 = f32[8,5120]{1,0:T(8,128)S(1)} fusion(bf16[1024,5120]{1,0:T(8,128)(2,1)} %param.27, bf16[8,5120]{1,0:T(8,128)(2,1)S(1)} %reshape.133, bf16[5120,1024]{1,0:T(8,128)(2,1)} %param.26, f32[8,1024]{1,0:T(8,128)S(1)} %fusion.61), kind=kOutput, calls=%fused_computation.42 | convolution fusion | flops 167821312 | bytes 21250048 | tf_op jit(solution)/shard_map/dot_general | solution.py:165
  412.5 5.9 %copy.99 = f32[4,2,5120]{0,1,2:T(2,128)} copy(f32[4,2,5120]{2,1,0:T(2,128)} %reshape.134) | data formatting | bytes 327680
  418.4 6.0 %reshape.161 = f32[5120,8]{1,0:T(8,128)} reshape(f32[5120,2,4]{2,1,0:T(2,128)} %bitcast.99) | data formatting | bytes 327680
  424.4 61.2 %reduce-scatter.4.cloned.1.call-done = f32[320,8]{1,0:T(8,128)} async-done(((f32[5120,8]{1,0:T(8,128)}), f32[320,8]{1,0:T(8,128)}) %reduce-scatter.4.cloned.1.call-update) | async-done | bytes 10256
  485.5 1.9 reshape.162
  (157 shorter events, 64.5 us)
Async XLA Ops:
  7.2 317.9 %copy-start = (bf16[5120,320]{0,1:T(8,128)(2,1)S(1)}, bf16[5120,320]{0,1:T(8,128)(2,1)}, u32[]{:S(2)}) copy-start(bf16[5120,320]{0,1:T(8,128)(2,1)} %param.23) | copy-start | bytes 9830404
  7.2 95.9 %all-reduce.3.cloned.1.call-start = ((), (), s32[]{:S(2)}) async-start(), calls=%async_computation.1 | async-start | bytes 327680 | tf_op jit(solution)/shard_map/psum | solution.py:88
  11.2 188.2 %all-reduce.5.cloned.1.call-start = ((), (), s32[]{:S(2)}) async-start(), calls=%async_computation.2 | async-start | bytes 458752 | tf_op jit(solution)/shard_map/psum | solution.py:93
  45.2 154.3 %copy-start.9 = (f32[7168]{0:T(1024)S(1)}, f32[7168]{0:T(1024)}, u32[]{:S(2)}) copy-start(f32[7168]{0:T(1024)} %param.20) | copy-start | bytes 86020
  109.1 154.3 %all-gather.5.cloned.1.call-start = ((), (), s32[]{:S(2)}) async-start(), calls=%async_computation.3 | async-start | bytes 2785280 | tf_op jit(solution)/shard_map/all_gather | solution.py:16
  200.4 0.7 copy-start.5
  201.1 6.5 %slice-start = ((s8[8388608]{0:T(1024)(128)(4,1)}), s8[4194304]{0:T(1024)(128)(4,1)S(1)}, s32[]{:S(2)}) async-start(s8[8388608]{0:T(1024)(128)(4,1)} %bitcast.102), calls=%async_computation.5 | async-start | bytes 8388608
  201.2 6.4 %copy-start.4 = (bf16[4,2,8,5,64]{4,3,0,2,1:T(8,128)(2,1)}, bf16[4,2,8,5,64]{4,3,0,2,1:T(8,128)(2,1)S(1)}, u32[]{:S(2)}) copy-start(bf16[4,2,8,5,64]{4,3,0,2,1:T(8,128)(2,1)S(1)} %copy.69) | copy-start | bytes 122884
  201.2 6.4 %slice-start.1 = ((s8[8388608]{0:T(1024)(128)(4,1)}), s8[4194304]{0:T(1024)(128)(4,1)S(1)}, s32[]{:S(2)}) async-start(s8[8388608]{0:T(1024)(128)(4,1)} %bitcast.102), calls=%async_computation.6 | async-start | bytes 8388608
  207.5 3.2 copy-start.1
  211.5 274.0 %reduce-scatter.4.cloned.1.call-start = ((), (), s32[]{:S(2)}) async-start(), calls=%async_computation.4 | async-start | bytes 2785280
  239.3 0.7 copy-start.2
  259.4 0.7 copy-start.3
  325.1 32.6 %copy-start.6 = (bf16[4,2,5120]{2,1,0:T(2,128)(2,1)}, bf16[4,2,5120]{2,1,0:T(2,128)(2,1)S(1)}, u32[]{:S(2)}) copy-start(bf16[4,2,5120]{2,1,0:T(2,128)(2,1)S(1)} %convert_element_type.77) | copy-start | bytes 245764
  327.0 30.7 %copy-start.7 = (f32[4,2,320]{2,1,0:T(2,128)}, f32[4,2,320]{2,1,0:T(2,128)S(1)}, u32[]{:S(2)}) copy-start(f32[4,2,320]{2,1,0:T(2,128)S(1)} %get-tuple-element.246) | copy-start | bytes 30724
  418.4 70.1 %copy-start.8 = (f32[4,2,320]{2,1,0:T(2,128)S(1)}, f32[4,2,320]{2,1,0:T(2,128)}, u32[]{:S(2)}) copy-start(f32[4,2,320]{2,1,0:T(2,128)} %copy-done.7) | copy-start | bytes 30724
Sparse Core Ops, SparseCore 0:
  11.4 91.6 all-reduce.2
  109.2 90.1 all-reduce.4
  211.6 46.0 all-gather.4
  424.5 61.0 reduce-scatter.3
where the time goes:
time: 499 us; the launch traced here: 496 us
  waiting for transfers between devices  209 us (42%)
  blocking collectives  106 us (21%)
  local copies, waits for them, and re-layouts  78.3 us (16%)
  other arithmetic  53.3 us (11%)
  matrix products  34 us (7%)
  between operations  14.1 us (3%)
    psum x1, waiting for transfers between devices, body(): joint_summed = lax.psum(joint_partial, 'seq')  90 us
    unnamed x5, waiting for transfers between devices  61.2 us
    psum x1, waiting for transfers between devices, body(): stream = lax.psum(partial_rows, 'seq')  57.9 us
    all_gather x2, blocking collectives, joined_2(): gathered = jax.tree.map(lambda a: lax.all_gather(a, axis), part)  42.5 us
    all_gather x1, blocking collectives, body(): normed_mid = lax.all_gather(normed_shard, 'seq', axis=2, tiled=True)  33.2 us
    unnamed x29, local copies, waits for them, and re-layouts  33.1 us
    psum x1, blocking collectives, body(): squares = lax.psum(jnp.sum(mid_shard * mid_shard, axis=-1), 'seq')  30.7 us
    add x15, other arithmetic, combine_partials(): sum_one * scale_one[..., None] + sum_two * scale_two[..., None]  27.3 us
  transfers between devices with their start and end apart: 4, of which 3 were waited for; matrix products, arithmetic and copies ran while one was open for 8% of the time, Pallas kernels for 0%

commit v1 on v0

--- a/solution.py
+++ b/solution.py
@@ -85,7 +85,7 @@
     inside = (local_ids >= 0) & (local_ids < vocab_rows)
     picked = jnp.take(embed_table, jnp.clip(local_ids, 0, vocab_rows - 1), axis=0)
     partial_rows = jnp.where(inside[..., None], picked.astype(jnp.float32), 0.0)
-    stream = lax.psum(partial_rows, "seq")
+    stream = jnp.sum(lax.all_gather(partial_rows, "seq"), axis=0)
     normed = rms_normalize(stream, attn_gain).reshape(-1, model_width)
     feature_rows = w_qkv.shape[0]
     normed_local = lax.dynamic_slice_in_dim(normed, rank * feature_rows, feature_rows, 1)

time: 499 us -> 452 us (0.906)
  waiting for transfers between devices: 209 us -> 164 us
    psum x1 -> x0, waiting for transfers between devices: 57.9 us -> none  [body(): stream = lax.psum(partial_rows, 'seq')]
    all_gather x0 -> x1, waiting for transfers between devices: none -> 14.6 us  [body(): stream = jnp.sum(lax.all_gather(partial_rows, 'seq'), axis=0)]
    unnamed x29 -> x35, local copies, waits for them, and re-layouts: 33.1 us -> 35.7 us
where the time goes in v1:
time: 452 us; the launch traced here: 450 us
  waiting for transfers between devices  164 us (36%)
  blocking collectives  106 us (23%)
  local copies, waits for them, and re-layouts  79.5 us (18%)
  other arithmetic  51.4 us (11%)
  matrix products  34 us (8%)
  between operations  14.1 us (3%)
    psum x1, waiting for transfers between devices, body(): joint_summed = lax.psum(joint_partial, 'seq')  87.9 us
    unnamed x5, waiting for transfers between devices  61.2 us
    all_gather x2, blocking collectives, joined_2(): gathered = jax.tree.map(lambda a: lax.all_gather(a, axis), part)  42.7 us
    unnamed x35, local copies, waits for them, and re-layouts  35.7 us
    all_gather x1, blocking collectives, body(): normed_mid = lax.all_gather(normed_shard, 'seq', axis=2, tiled=True)  33.6 us
    psum x1, blocking collectives, body(): squares = lax.psum(jnp.sum(mid_shard * mid_shard, axis=-1), 'seq')  30.2 us
    add x15, other arithmetic, combine_partials(): sum_one * scale_one[..., None] + sum_two * scale_two[..., None]  27.3 us
    dynamic_slice x18, local copies, waits for them, and re-layouts, take(): lax.dynamic_index_in_dim(a, source, 0, False)  14.9 us
  transfers between devices with their start and end apart: 4, of which 3 were waited for; matrix products, arithmetic and copies ran while one was open for 8% of the time, Pallas kernels for 0%

profile of v1, /device:TPU:0, one launch (start us, length us, event | category | flops | bytes accessed | tf_op | source)
XLA Modules:
  0.0 449.6 jit_solution(5400480129607817109)
XLA Ops:
  8.3 1.9 gather_fusion
  11.0 8.8 %copy.152 = bf16[512,8,8,128]{3,2,1,0:T(8,128)(2,1)} copy(bf16[512,8,8,128]{3,1,2,0:T(8,128)(2,1)} %bitcast.100) | data formatting | bytes 16777216
  19.8 9.0 %copy.153 = bf16[512,8,8,128]{3,2,1,0:T(8,128)(2,1)} copy(bf16[512,8,8,128]{3,1,2,0:T(8,128)(2,1)} %bitcast.101) | data formatting | bytes 16777216
  29.7 7.5 %bitcast_bitcast_fusion.1 = bf16[2,2048,8,128,1]{3,2,1,0,4:T(8,128)(2,1)} fusion(bf16[2,2048,8,128]{3,2,1,0:T(8,128)(2,1)} %bitcast.98), kind=kLoop, calls=%fused_computation.12 | loop fusion | bytes 16777216 | tf_op jit(solution)/shard_map/reshape | solution.py:108
  38.7 3.6 bitcast_bitcast_fusion
  42.2 14.6 %all-gather.6.cloned.1.call-done = f32[16,4,2,5120]{3,1,2,0:T(4,128)} async-done(((f32[1,4,2,5120]{3,1,2,0:T(4,128)}), f32[16,4,2,5120]{3,1,2,0:T(4,128)}) %all-gather.6.cloned.1.call-update) | async-done | bytes 2621456 | tf_op jit(solution)/shard_map/all_gather | solution.py:88
  56.8 2.2 reduce_sum.47
  61.2 3.7 fusion.49
  65.3 87.9 %all-reduce.2.cloned.1.call-done = f32[8,7168]{1,0:T(8,128)} async-done(((f32[8,7168]{1,0:T(8,128)}), f32[8,7168]{1,0:T(8,128)}) %all-reduce.2.cloned.1.call-update) | async-done | bytes 229392 | tf_op jit(solution)/shard_map/psum | solution.py:93
  154.9 6.3 %bitcast_reduce_fusion = (f32[2,8,5,4]{2,3,1,0:T(4,128)S(1)}, f32[2,8,4,5,2048]{4,3,2,1,0:T(8,128)S(1)}) fusion(pred[2,2048]{1,0:T(4,128)(4,1)S(1)} %broadcast_compare_fusion, bf16[2,2048,8,128,1]{3,2,1,0,4:T(8,128)(2,1)} %bitcast_bitcast_fusion.1, bf16[4,2,8,5,64]{4,3,0,2,1:T(8,128)(2,1)S(1)} %copy.111, bf16[4,2,8,5,64]{4,3,0,2,1:T(8,128)(2,1)S(1)} %copy.110), kind=kOutput, calls=%fused_computation.18 | convolution fusion | flops 169901760 | bytes 11097344 | tf_op jit(solution)/shard_map/sbkgd,bpkd->bkgsp/dot_general | solution.py:111
  161.3 3.1 fusion.4
  165.5 3.6 fusion.13
  169.2 22.9 %all-gather.1 = f32[32,8,5,4]{1,3,2,0:T(4,128)S(1)} all-gather(f32[2,8,5,4]{1,3,2,0:T(4,128)S(1)} %copy.114), channel_id=3, replica_groups=mesh['parts'=2,'seq'=16] {'seq'}, dimensions={0}, use_global_device_ids=true | all-gather | bytes 21760 | tf_op jit(solution)/shard_map/all_gather | solution.py:16
  192.8 19.8 %all-gather = f32[32,8,5,4]{1,3,2,0:T(4,128)S(1)} all-gather(f32[2,8,5,4]{1,3,2,0:T(4,128)S(1)} %copy.113), channel_id=2, replica_groups=mesh['parts'=2,'seq'=16] {'seq'}, dimensions={0}, use_global_device_ids=true | all-gather | bytes 21760 | tf_op jit(solution)/shard_map/all_gather | solution.py:16
  214.3 2.3 fusion.64
  218.3 57.2 %while.19 = (s32[]{:T(128)}, f32[2,8,5,4]{1,3,2,0:T(4,128)S(1)}, f32[2,8,5,4]{1,3,2,0:T(4,128)S(1)}, f32[2,8,5,4,128]{4,3,2,1,0:T(4,128)}, f32[16,2,8,5,4]{2,4,3...) while((s32[]{:T(128)}, f32[2,8,5,4]{1,3,2,0:T(4,128)S(1)}, ...), condition=%wide.region_6.7_spmd, body=%wide.region_5.6_spmd.sunk | while | flops 124805 | bytes 837271 | solution.py:21
  220.2 1.8 fusion.76
  224.1 1.8 fusion.76
  227.9 1.8 fusion.76
  231.7 1.8 fusion.76
  235.5 1.8 fusion.76
  254.6 1.8 fusion.76
  278.3 1.8 multiply_reduce_fusion.1
  281.0 30.2 %psum.15 = f32[4,2]{0,1:T(2,128)S(1)} all-reduce(f32[4,2]{0,1:T(2,128)S(1)} %copy.149), channel_id=1, replica_groups=mesh['parts'=2,'seq'=16] {'seq'}, use_global_device_ids=true, to_apply=%region_10.11 | all-reduce | flops 8 | bytes 64 | tf_op jit(solution)/shard_map/psum | solution.py:154
  311.5 33.6 %all_gather.32 = bf16[4,2,5120]{0,1,2:T(2,128)(2,1)} all-gather(bf16[4,2,320]{0,1,2:T(2,128)(2,1)S(1)} %copy.129), channel_id=1, replica_groups=mesh['parts'=2,'seq'=16] {'seq'}, dimensions={2}, use_global_device_ids=true | all-gather | bytes 87040 | tf_op jit(solution)/shard_map/all_gather | solution.py:160
  345.2 5.2 %copy.130 = bf16[4,2,5120]{2,1,0:T(2,128)(2,1)S(1)} copy(bf16[4,2,5120]{0,1,2:T(2,128)(2,1)} %all_gather.32) | data formatting | bytes 163840 | tf_op jit(solution)/shard_map/all_gather | solution.py:160
  350.4 5.4 %fusion.65 = f32[8,1024]{1,0:T(8,128)S(1)} fusion(bf16[8,5120]{1,0:T(8,128)(2,1)S(1)} %reshape.152, bf16[5120,1024]{1,0:T(8,128)(2,1)} %param.25), kind=kOutput, calls=%fused_computation.108 | convolution fusion | flops 83886080 | bytes 10600448 | tf_op jit(solution)/shard_map/dot_general | solution.py:162
  355.9 9.8 %fusion.30 = f32[8,5120]{1,0:T(8,128)S(1)} fusion(bf16[1024,5120]{1,0:T(8,128)(2,1)} %param.27, bf16[8,5120]{1,0:T(8,128)(2,1)S(1)} %reshape.152, bf16[5120,1024]{1,0:T(8,128)(2,1)} %param.26, f32[8,1024]{1,0:T(8,128)S(1)} %fusion.65), kind=kOutput, calls=%fused_computation.42 | convolution fusion | flops 167821312 | bytes 21250048 | tf_op jit(solution)/shard_map/dot_general | solution.py:165
  366.4 5.9 %copy.143 = f32[4,2,5120]{0,1,2:T(2,128)} copy(f32[4,2,5120]{2,1,0:T(2,128)} %reshape.153) | data formatting | bytes 327680
  372.4 6.0 %reshape.181 = f32[5120,8]{1,0:T(8,128)} reshape(f32[5120,2,4]{2,1,0:T(2,128)} %bitcast.99) | data formatting | bytes 327680
  378.4 61.1 %reduce-scatter.4.cloned.1.call-done = f32[320,8]{1,0:T(8,128)} async-done(((f32[5120,8]{1,0:T(8,128)}), f32[320,8]{1,0:T(8,128)}) %reduce-scatter.4.cloned.1.call-update) | async-done | bytes 10256
  439.5 1.9 reshape.182
  (164 shorter events, 66.4 us)
Async XLA Ops:
  7.2 271.1 %copy-start = (bf16[5120,320]{0,1:T(8,128)(2,1)S(1)}, bf16[5120,320]{0,1:T(8,128)(2,1)}, u32[]{:S(2)}) copy-start(bf16[5120,320]{0,1:T(8,128)(2,1)} %param.23) | copy-start | bytes 9830404
  7.2 49.6 %all-gather.6.cloned.1.call-start = ((), (), s32[]{:S(2)}) async-start(), calls=%async_computation.1 | async-start | bytes 2785280 | tf_op jit(solution)/shard_map/all_gather | solution.py:88
  11.0 142.2 %all-reduce.2.cloned.1.call-start = ((), (), s32[]{:S(2)}) async-start(), calls=%async_computation.2 | async-start | bytes 458752 | tf_op jit(solution)/shard_map/psum | solution.py:93
  19.8 9.7 %copy-start.11 = (s32[2]{0:T(128)S(1)}, s32[2]{0:T(128)}, u32[]{:S(2)}) copy-start(s32[2]{0:T(128)} %param.16) | copy-start | bytes 28
  29.7 9.0 %copy-start.1 = (bf16[512,8,8,128]{3,2,1,0:T(8,128)(2,1)S(1)}, bf16[512,8,8,128]{3,2,1,0:T(8,128)(2,1)}, u32[]{:S(2)}) copy-start(bf16[512,8,8,128]{3,2,1,0:T(8,128)(2,1)} %copy.153) | copy-start | bytes 25165828
  42.2 111.0 %copy-start.10 = (f32[7168]{0:T(1024)S(1)}, f32[7168]{0:T(1024)}, u32[]{:S(2)}) copy-start(f32[7168]{0:T(1024)} %param.20) | copy-start | bytes 86020
  64.9 151.7 %all-gather.8.cloned.1.call-start = ((), (), s32[]{:S(2)}) async-start(), calls=%async_computation.3 | async-start | bytes 2785280 | tf_op jit(solution)/shard_map/all_gather | solution.py:16
  154.2 0.7 copy-start.6
  154.9 6.5 %slice-start = ((s8[8388608]{0:T(1024)(128)(4,1)}), s8[4194304]{0:T(1024)(128)(4,1)S(1)}, s32[]{:S(2)}) async-start(s8[8388608]{0:T(1024)(128)(4,1)} %bitcast.102), calls=%async_computation.5 | async-start | bytes 8388608
  154.9 6.4 %copy-start.5 = (bf16[4,2,8,5,64]{4,3,0,2,1:T(8,128)(2,1)}, bf16[4,2,8,5,64]{4,3,0,2,1:T(8,128)(2,1)S(1)}, u32[]{:S(2)}) copy-start(bf16[4,2,8,5,64]{4,3,0,2,1:T(8,128)(2,1)S(1)} %copy.111) | copy-start | bytes 122884
  154.9 6.4 %slice-start.1 = ((s8[8388608]{0:T(1024)(128)(4,1)}), s8[4194304]{0:T(1024)(128)(4,1)S(1)}, s32[]{:S(2)}) async-start(s8[8388608]{0:T(1024)(128)(4,1)} %bitcast.102), calls=%async_computation.6 | async-start | bytes 8388608
  161.3 3.2 copy-start.2
  165.3 274.2 %reduce-scatter.4.cloned.1.call-start = ((), (), s32[]{:S(2)}) async-start(), calls=%async_computation.4 | async-start | bytes 2785280
  192.1 0.7 copy-start.3
  212.6 0.7 copy-start.4
  278.3 33.0 %copy-start.7 = (bf16[4,2,5120]{2,1,0:T(2,128)(2,1)}, bf16[4,2,5120]{2,1,0:T(2,128)(2,1)S(1)}, u32[]{:S(2)}) copy-start(bf16[4,2,5120]{2,1,0:T(2,128)(2,1)S(1)} %convert_element_type.85) | copy-start | bytes 245764
  280.1 31.1 %copy-start.8 = (f32[4,2,320]{2,1,0:T(2,128)}, f32[4,2,320]{2,1,0:T(2,128)S(1)}, u32[]{:S(2)}) copy-start(f32[4,2,320]{2,1,0:T(2,128)S(1)} %get-tuple-element.253) | copy-start | bytes 30724
  372.4 70.1 %copy-start.9 = (f32[4,2,320]{2,1,0:T(2,128)S(1)}, f32[4,2,320]{2,1,0:T(2,128)}, u32[]{:S(2)}) copy-start(f32[4,2,320]{2,1,0:T(2,128)} %copy-done.8) | copy-start | bytes 30724
Sparse Core Ops, SparseCore 0:
  11.1 45.6 all-gather.5
  65.1 88.0 all-reduce.1
  165.4 45.4 all-gather.7
  378.5 60.9 reduce-scatter.3
